TPU v7x, 64 devices: a 2x2x8 block of a 4x4x8 slice. The times are simulated.
64 devices in a mesh: rep: 8 (over x, y, core), dp: 8 (over z).
Axes of the slice: x: 2, y: 2, z: 8, core: 2. Of those that a mesh axis runs over, the one named last changes fastest.
The devices are a block of a 4x4x8 slice.
Arguments:
- x: bfloat16 [64, 2048, 768], P(('rep', 'dp')), parts along dimension 0
- dy: bfloat16 [64, 2048, 768], P(('rep', 'dp')), parts along dimension 0
- w_gate: bfloat16 [2, 768, 2048], replicated
- w_up: bfloat16 [2, 768, 2048], replicated
- w_down: bfloat16 [2, 2048, 768], replicated
- m_w_gate: float32 [2, 768, 2048], replicated
- m_w_up: float32 [2, 768, 2048], replicated
- m_w_down: float32 [2, 2048, 768], replicated
- v_w_gate: float32 [2, 768, 2048], replicated
- v_w_up: float32 [2, 768, 2048], replicated
- v_w_down: float32 [2, 2048, 768], replicated
Outputs:
- output 1: bfloat16 [16, 768, 2048], P('rep'), parts along dimension 0
- output 2: bfloat16 [16, 768, 2048], P('rep'), parts along dimension 0
- output 3: bfloat16 [16, 2048, 768], P('rep'), parts along dimension 0
- output 4: float32 [16, 768, 2048], P('rep'), parts along dimension 0
- output 5: float32 [16, 768, 2048], P('rep'), parts along dimension 0
- output 6: float32 [16, 2048, 768], P('rep'), parts along dimension 0
- output 7: float32 [16, 768, 2048], P('rep'), parts along dimension 0
- output 8: float32 [16, 768, 2048], P('rep'), parts along dimension 0
- output 9: float32 [16, 2048, 768], P('rep'), parts along dimension 0
There are 8 independent parts. A program takes and returns all parts, laid end to end along the dimension named above; an argument that names none is the same for every part.
All inputs are finite; a program needn't handle non-finite values.
Results may differ from a plain program's by a relative error of at most 0.02.
Values are sent between devices in bfloat16 or wider.
A program may use at most 768 MiB of HBM per device.

v0:
```python
import jax
import jax.numpy as jnp
from jax import lax
from jax.sharding import PartitionSpec as P

NAMES = ("w_gate", "w_up", "w_down")


def matmul(a, w):
    return jnp.dot(a, w, preferred_element_type=jnp.float32).astype(jnp.bfloat16)


def normed(h):
    wide = h.astype(jnp.float32)
    scale = lax.rsqrt(jnp.mean(wide**2, -1, keepdims=True) + 1e-6)
    return (wide * scale).astype(jnp.bfloat16)


def layer(h, w):
    a = normed(h)
    gate = jnp.dot(a, w["w_gate"], preferred_element_type=jnp.float32)
    up = jnp.dot(a, w["w_up"], preferred_element_type=jnp.float32)
    return h + matmul((jax.nn.silu(gate) * up).astype(jnp.bfloat16), w["w_down"])


def adamw(w, m, v, g):
    m = 0.9 * m + 0.1 * g
    v = 0.95 * v + 0.05 * g * g
    step = m * lax.rsqrt(v + 1e-8) + 0.1 * w
    return (w - 0.02 * step).astype(jnp.bfloat16), m, v


def solution(mesh):
    def step(x, dy, *arrays):
        weights, m, v = (arrays[i : i + 3] for i in (0, 3, 6))
        layers = weights[0].shape[0]
        h, kept = x[0], []
        for number in range(layers):
            kept.append(h)
            h = layer(h, {name: w[number] for name, w in zip(NAMES, weights, strict=True)})
        by_h, summed = dy[0], [None] * layers
        for number in reversed(range(layers)):
            _, back = jax.vjp(lambda w, h: layer(h, w), {name: w[number] for name, w in zip(NAMES, weights, strict=True)}, kept[number])
            by_w, by_h = back(by_h)
            summed[number] = [lax.psum(by_w[name], "dp") for name in NAMES]
        gradients = [jnp.stack([summed[number][i] for number in range(layers)]).astype(jnp.float32) for i in range(3)]
        new = [adamw(w.astype(jnp.float32), m, v, g) for w, m, v, g in zip(weights, m, v, gradients, strict=True)]
        return tuple(one[which] for which in range(3) for one in new)

    return jax.shard_map(
        step,
        mesh=mesh,
        in_specs=(P(("rep", "dp"), None, None),) * 2 + (P(None, None, None),) * 9,
        out_specs=(P("rep", None, None),) * 9,
        check_vma=False,
    )
```

profile of v0, /device:TPU:21, one launch (start us, length us, event | category | flops | bytes accessed | tf_op | source)
XLA Modules:
  0.0 689.1 jit_solution(12146990781744420790)
XLA Ops:
  7.2 0.1 all-reduce.3.cloned.1.call-start
  7.3 3.2 copy.20
  10.5 0.7 fusion.30
  11.2 5.0 copy.21
  16.2 11.5 %convolution_convert_fusion.1 = bf16[2048,2048]{1,0:T(8,128)(2,1)} fusion(bf16[1,2048,768]{2,1,0:T(8,128)(2,1)} %param.12, bf16[2,2048,768]{2,1,0:T(8,128)(2,1)} %param.15), kind=kOutput, calls=%fused_computation.59 | convolution fusion | flops 6446645248 | bytes 14680064 | tf_op jit(solution)/shard_map/transpose(jvp())/dot_general | solution.py:10
  27.7 11.8 %fusion.59 = f32[2048,2048]{1,0:T(8,128)} fusion(bf16[2,768,2048]{2,1,0:T(8,128)(2,1)} %param.13, bf16[1,2048,768]{2,1,0:T(8,128)(2,1)S(1)} %copy-done.3, f32[2048]{0:T(1024)S(1)} %add_rsqrt_fusion), kind=kOutput, calls=%fused_computation.95 | convolution fusion | flops 6447169536 | bytes 23076864 | tf_op jit(solution)/shard_map/dot_general | solution.py:21
  39.5 17.1 %multiply_convert_fusion.1 = (bf16[2048,2048]{1,0:T(8,128)(2,1)}, f32[2048,2048]{1,0:T(8,128)}) fusion(f32[2048,2048]{1,0:T(8,128)} %fusion.59, bf16[2,768,2048]{2,1,0:T(8,128)(2,1)} %param.14, bf16[1,2048,768]{2,1,0:T(8,128)(2,1)} %param.11, f32[2048]{0:T(1024)S(1)} %add_rsqrt_fusion), kind=kOutput, calls=%fused_computation.20 | convolution fusion | flops 6472335360 | bytes 48242688 | tf_op jit(solution)/shard_map/dot_general | solution.py:22
  56.6 10.8 %fusion.34 = (f32[2048]{0:T(1024)S(1)}, bf16[2048,768]{0,1:T(8,128)(2,1)S(1)}) fusion(bf16[2048,2048]{1,0:T(8,128)(2,1)} %get-tuple-element.24, bf16[2,2048,768]{2,1,0:T(8,128)(2,1)} %param.15, bf16[1,2048,768]{1,2,0:T(8,128)(2,1)S(1)} %copy.20), kind=kOutput, calls=%fused_computation.64 | convolution fusion | flops 6450313216 | bytes 17833984 | tf_op jit(solution)/shard_map/dot_general | solution.py:10
  67.5 1.6 copy-done.5
  69.1 12.1 %fusion.48 = f32[2048,2048]{1,0:T(8,128)} fusion(bf16[2,768,2048]{2,1,0:T(8,128)(2,1)} %param.14, bf16[2048,768]{0,1:T(8,128)(2,1)S(1)} %get-tuple-element.27, f32[2048]{0:T(1024)S(1)} %fusion.94), kind=kOutput, calls=%fused_computation.84 | convolution fusion | flops 6447169536 | bytes 23076864 | tf_op jit(solution)/shard_map/jvp()/dot_general | solution.py:22
  81.2 27.4 %fusion.2 = (bf16[2048,2048]{1,0:T(8,128)(2,1)}, f32[2048,2048]{1,0:T(8,128)}) fusion(f32[2048,2048]{1,0:T(8,128)} %fusion.48, bf16[2048,2048]{1,0:T(8,128)(2,1)} %convolution_convert_fusion.1, bf16[2,768,2048]{2,1,0:T(8,128)(2,1)} %param.13, bf16[2048,768]{0,1:T(8,128)(2,1)} %copy-done.5, f32[2048]{0:T(1024)S(1)} %fusion.94), kind=kOutput, calls=%fused_computation.11 | convolution fusion | flops 6497501184 | bytes 56631296 | tf_op jit(solution)/shard_map/jvp()/dot_general | solution.py:21
  108.6 10.3 %fusion.71 = bf16[1,768,2048]{2,1,0:T(8,128)(2,1)} fusion(bf16[2048,2048]{1,0:T(8,128)(2,1)} %get-tuple-element.28, bf16[2048,768]{0,1:T(8,128)(2,1)S(1)} %copy-done.6, f32[2048]{0:T(1024)S(1)} %fusion.94), kind=kOutput, calls=%fused_computation.104 | convolution fusion | flops 6447169536 | bytes 14688256 | tf_op jit(solution)/shard_map/transpose(jvp())/dot_general | solution.py:21
  118.9 9.7 %convolution_convert_fusion.3 = bf16[2048,768]{0,1:T(8,128)(2,1)} fusion(bf16[2048,2048]{1,0:T(8,128)(2,1)S(1)} %copy-done.11, bf16[2,768,2048]{2,1,0:T(8,128)(2,1)} %param.13), kind=kOutput, calls=%fused_computation.74 | convolution fusion | flops 6442450944 | bytes 14680064 | tf_op jit(solution)/shard_map/transpose(jvp())/dot_general | solution.py:21
  128.6 16.1 %fusion.68 = bf16[1,2048,768]{2,1,0:T(8,128)(2,1)} fusion(bf16[1,2048,768]{2,1,0:T(8,128)(2,1)S(1)} %copy-done.4, f32[2048,2048]{1,0:T(8,128)} %fusion.48, f32[2048,2048]{1,0:T(8,128)} %get-tuple-element.29), kind=kOutput, calls=%fused_computation.103 | convolution fusion | flops 6469189632 | bytes 39845888 | tf_op jit(solution)/shard_map/transpose(jvp())/dot_general | solution.py:10
  144.7 12.9 %fusion.73 = bf16[1,768,2048]{2,1,0:T(8,128)(2,1)} fusion(bf16[2048,2048]{1,0:T(8,128)(2,1)} %convolution_convert_fusion.1, bf16[2048,768]{0,1:T(8,128)(2,1)S(1)} %copy-done.6, f32[2048]{0:T(1024)S(1)} %fusion.94, f32[2048,2048]{1,0:T(8,128)} %get-tuple-element.29), kind=kOutput, calls=%fused_computation.106 | convolution fusion | flops 6473908224 | bytes 31465472 | tf_op jit(solution)/shard_map/transpose(jvp())/dot_general | solution.py:22
  157.7 17.9 %fusion.36 = (f32[2048]{0:T(1024)S(1)}, bf16[2048,768]{0,1:T(8,128)(2,1)}) fusion(bf16[2048,768]{0,1:T(8,128)(2,1)} %copy-done.5, bf16[2048,768]{0,1:T(8,128)(2,1)} %convolution_convert_fusion.3, bf16[2,768,2048]{2,1,0:T(8,128)(2,1)} %param.14, bf16[2048,2048]{1,0:T(8,128)(2,1)} %convolution_convert_fusion.1, f32[2048,2048]{1,0:T(8,128)} %get-tuple-element.29), kind=kOutput, calls=%fused_computation.66 | convolution fusion | flops 6477051904 | bytes 37756928 | tf_op jit(solution)/shard_map/transpose(jvp())/dot_general | solution.py:22
  175.7 5.2 fusion.45
  180.9 10.6 %fusion.64 = bf16[1,2048,768]{2,1,0:T(8,128)(2,1)} fusion(bf16[2048,2048]{1,0:T(8,128)(2,1)} %get-tuple-element.24, bf16[2048,768]{0,1:T(8,128)(2,1)S(1)} %fusion.45), kind=kOutput, calls=%fused_computation.101 | convolution fusion | flops 6444023808 | bytes 14680064 | tf_op jit(solution)/shard_map/transpose(jvp())/dot_general | solution.py:10
  191.5 7.1 %convolution_convert_fusion = bf16[2048,2048]{1,0:T(8,128)(2,1)S(1)} fusion(bf16[2048,768]{0,1:T(8,128)(2,1)S(1)} %fusion.45, bf16[2,2048,768]{2,1,0:T(8,128)(2,1)S(1)} %bitcast.79), kind=kOutput, calls=%fused_computation.58 | convolution fusion | flops 6446645248 | bytes 14680064 | tf_op jit(solution)/shard_map/transpose(jvp())/dot_general | solution.py:10
  198.7 14.7 %fusion.72 = bf16[1,768,2048]{2,1,0:T(8,128)(2,1)} fusion(bf16[2048,2048]{1,0:T(8,128)(2,1)S(1)} %convolution_convert_fusion, f32[2048,2048]{1,0:T(8,128)} %fusion.59, bf16[1,2048,768]{1,2,0:T(8,128)(2,1)S(1)} %copy-done.1, f32[2048]{0:T(1024)S(1)} %copy-done.10), kind=kOutput, calls=%fused_computation.105 | convolution fusion | flops 6473908224 | bytes 31465472 | tf_op jit(solution)/shard_map/transpose(jvp())/dot_general | solution.py:22
  213.3 19.0 %fusion.65 = bf16[1,768,2048]{2,1,0:T(8,128)(2,1)} fusion(f32[2048,2048]{1,0:T(8,128)} %fusion.59, f32[2048,2048]{1,0:T(8,128)} %get-tuple-element.25, bf16[2048,2048]{1,0:T(8,128)(2,1)} %copy-done.12, bf16[1,2048,768]{1,2,0:T(8,128)(2,1)S(1)} %copy-done.1, f32[2048]{0:T(1024)S(1)} %copy-done.10), kind=kOutput, calls=%fused_computation.102 | convolution fusion | flops 6494879744 | bytes 48242688 | tf_op jit(solution)/shard_map/transpose(jvp())/dot_general | solution.py:21
  232.4 382.6 %all-reduce.3.cloned.1.call-done = (bf16[1,768,2048]{2,1,0:T(8,128)(2,1)}, bf16[1,768,2048]{2,1,0:T(8,128)(2,1)}, bf16[1,768,2048]{2,1,0:T(8,128)(2,1)}, bf16[1,...) async-done(((bf16[1,768,2048]{2,1,0:T(8,128)(2,1)}, bf16[1,768,2048]{2,1,0:T(8,128)(2,1)}, bf16[1,768,2048]{2,1,0:T(8,128)(2,1)}, ...) | async-done | bytes 18874384 | tf_op jit(solution)/shard_map/psum | solution.py:45
  615.0 24.5 %fusion.21 = (bf16[2,2048,768]{2,1,0:T(8,128)(2,1)}, f32[2,2048,768]{2,1,0:T(8,128)}, f32[2,2048,768]{2,1,0:T(8,128)}) fusion(bf16[2,2048,768]{2,1,0:T(8,128)(2,1)} %param.15, bf16[1,2048,768]{2,1,0:T(8,128)(2,1)} %get-tuple-element.13, bf16[1,2048,768]{2,1,0:T(8,128)(2,1)} %get-tuple-element.14, f32[2,2048,768]{2,1,0:T(8,128)} %param.21, ...), kind=kLoop, calls=%fused_computation.42 | loop fusion | flops 59768832 | bytes 69206016 | tf_op jit(solution)/shard_map/convert_element_type | solution.py:30
  639.6 42.1 %fusion.13 = (bf16[2,768,2048]{2,1,0:T(8,128)(2,1)}, f32[2,768,2048]{2,1,0:T(8,128)}, f32[2,768,2048]{2,1,0:T(8,128)}, bf16[2,768,2048]{2,1,0:T(8,128)(2,1)}, f3...) fusion(bf16[2,768,2048]{2,1,0:T(8,128)(2,1)S(1)} %bitcast.77, bf16[1,768,2048]{2,1,0:T(8,128)(2,1)} %get-tuple-element.9, ...), kind=kLoop, calls=%fused_computation.34 | loop fusion | flops 119537664 | bytes 138412032 | tf_op jit(solution)/shard_map/convert_element_type | solution.py:30
  (39 shorter events, 0.2 us)
Async XLA Ops:
  7.2 607.8 %all-reduce.3.cloned.1.call-start = ((), (), s32[]{:S(2)}) async-start(), calls=%async_computation | async-start | bytes 37748736 | tf_op jit(solution)/shard_map/psum | solution.py:45
  10.5 46.1 %copy-start = (bf16[1,2048,768]{1,2,0:T(8,128)(2,1)}, bf16[1,2048,768]{1,2,0:T(8,128)(2,1)S(1)}, u32[]{:S(2)}) copy-start(bf16[1,2048,768]{1,2,0:T(8,128)(2,1)S(1)} %copy.20) | copy-start | bytes 9437188
  11.1 28.3 %copy-start.9 = (f32[2048]{0:T(1024)}, f32[2048]{0:T(1024)S(1)}, u32[]{:S(2)}) copy-start(f32[2048]{0:T(1024)S(1)} %add_rsqrt_fusion) | copy-start | bytes 24580
  16.2 11.5 %copy-start.3 = (bf16[1,2048,768]{2,1,0:T(8,128)(2,1)S(1)}, bf16[1,2048,768]{2,1,0:T(8,128)(2,1)}, u32[]{:S(2)}) copy-start(bf16[1,2048,768]{2,1,0:T(8,128)(2,1)} %param.11) | copy-start | bytes 9437188
  67.4 1.7 copy-start.5
  67.4 1.7 copy-start.7
  81.2 27.4 %copy-start.6 = (bf16[2048,768]{0,1:T(8,128)(2,1)S(1)}, bf16[2048,768]{0,1:T(8,128)(2,1)}, u32[]{:S(2)}) copy-start(bf16[2048,768]{0,1:T(8,128)(2,1)} %copy-done.5) | copy-start | bytes 9437188
  108.6 10.3 %copy-start.11 = (bf16[2048,2048]{1,0:T(8,128)(2,1)S(1)}, bf16[2048,2048]{1,0:T(8,128)(2,1)}, u32[]{:S(2)}) copy-start(bf16[2048,2048]{1,0:T(8,128)(2,1)} %get-tuple-element.28) | copy-start | bytes 25165828
  118.9 9.7 %copy-start.4 = (bf16[1,2048,768]{2,1,0:T(8,128)(2,1)S(1)}, bf16[1,2048,768]{2,1,0:T(8,128)(2,1)}, u32[]{:S(2)}) copy-start(bf16[1,2048,768]{2,1,0:T(8,128)(2,1)} %param.12) | copy-start | bytes 9437188
  157.7 17.9 %copy-start.8 = (f32[2048]{0:T(1024)S(1)}, f32[2048]{0:T(1024)}, u32[]{:S(2)}) copy-start(f32[2048]{0:T(1024)} %copy-done.7) | copy-start | bytes 24580
  157.7 18.0 %copy-start.2 = (bf16[1,2048,768]{1,2,0:T(8,128)(2,1)S(1)}, bf16[1,2048,768]{1,2,0:T(8,128)(2,1)}, u32[]{:S(2)}) copy-start(bf16[1,2048,768]{1,2,0:T(8,128)(2,1)} %copy.21) | copy-start | bytes 9437188
  175.7 15.8 %slice-start.2 = ((s8[6291456]{0:T(1024)(128)(4,1)}), s8[2097152]{0:T(1024)(128)(4,1)S(1)}, s32[]{:S(2)}) async-start(s8[6291456]{0:T(1024)(128)(4,1)} %bitcast.78), calls=%async_computation.3 | async-start | bytes 4194304
  180.9 10.6 %slice-start.3 = ((s8[6291456]{0:T(1024)(128)(4,1)}), s8[4194304]{0:T(1024)(128)(4,1)S(1)}, s32[]{:S(2)}) async-start(s8[6291456]{0:T(1024)(128)(4,1)} %bitcast.78), calls=%async_computation.4 | async-start | bytes 8388608
  191.5 7.1 %copy-start.1 = (bf16[1,2048,768]{1,2,0:T(8,128)(2,1)S(1)}, bf16[1,2048,768]{1,2,0:T(8,128)(2,1)}, u32[]{:S(2)}) copy-start(bf16[1,2048,768]{1,2,0:T(8,128)(2,1)} %copy-done) | copy-start | bytes 9437188
  191.5 7.1 %copy-start.10 = (f32[2048]{0:T(1024)S(1)}, f32[2048]{0:T(1024)}, u32[]{:S(2)}) copy-start(f32[2048]{0:T(1024)} %copy-done.9) | copy-start | bytes 24580
  198.7 14.7 %copy-start.12 = (bf16[2048,2048]{1,0:T(8,128)(2,1)}, bf16[2048,2048]{1,0:T(8,128)(2,1)S(1)}, u32[]{:S(2)}) copy-start(bf16[2048,2048]{1,0:T(8,128)(2,1)S(1)} %convolution_convert_fusion) | copy-start | bytes 25165828
  232.4 407.2 %slice-start = ((s8[6291456]{0:T(1024)(128)(4,1)}), s8[2097152]{0:T(1024)(128)(4,1)S(1)}, s32[]{:S(2)}) async-start(s8[6291456]{0:T(1024)(128)(4,1)} %bitcast.76), calls=%async_computation.1 | async-start | bytes 4194304
  615.0 24.6 %slice-start.1 = ((s8[6291456]{0:T(1024)(128)(4,1)}), s8[4194304]{0:T(1024)(128)(4,1)S(1)}, s32[]{:S(2)}) async-start(s8[6291456]{0:T(1024)(128)(4,1)} %bitcast.76), calls=%async_computation.2 | async-start | bytes 8388608
Sparse Core Ops, SparseCore 0:
  232.5 382.4 all-reduce.2
where the time goes:
time: 696 us; the launch traced here: 689 us
  waiting for transfers between devices  383 us (55%)
  matrix products  209 us (30%)
  other arithmetic  72.6 us (10%)
  between operations  14.8 us (2%)
  local copies, waits for them, and re-layouts  9.93 us (1%)
    psum x1, waiting for transfers between devices, step(): summed[number] = [lax.psum(by_w[name], 'dp') for name in NAMES]  383 us
    dot_general x5, matrix products, layer(): gate = jnp.dot(a, w['w_gate'], preferred_element_type=jnp.float32)  78.2 us
    dot_general x5, matrix products, layer(): up = jnp.dot(a, w['w_up'], preferred_element_type=jnp.float32)  74.8 us
    convert_element_type x2, other arithmetic, adamw(): return ((w - 0.02 * step).astype(jnp.bfloat16), m, v)  66.7 us
    dot_general x5, matrix products, matmul(): jnp.dot(a, w, preferred_element_type=jnp.float32).astype(jnp.bfloat16)  56.2 us
  transfers between devices with their start and end apart: 1, of which 1 were waited for; matrix products, arithmetic and copies ran while one was open for 0% of the time, Pallas kernels for 0%

commit v1 on v0

v1 whole, which is shorter than its diff:
```python
import functools

import jax
import jax.numpy as jnp
from jax import lax
from jax.experimental import pallas as pl
from jax.experimental.pallas import tpu as pltpu
from jax.sharding import PartitionSpec as P

F32, BF16 = jnp.float32, jnp.bfloat16
LIMIT = 60 * 1024 * 1024
ROWS = 512
CUT = 512
TILE = 256
DIRECT = 2
NT = (((1,), (1,)), ((), ()))


def dot(a, b):
    return jnp.dot(a, b, preferred_element_type=F32)


def dot_nt(a, b):
    return lax.dot_general(a, b, NT, preferred_element_type=F32)


def scale_of(wide):
    return lax.rsqrt(jnp.mean(wide * wide, -1, keepdims=True) + 1e-6)


def forward_kernel(x_ref, dy_ref, wg_ref, wu_ref, wd_ref, h_ref, a1_ref, a1t_ref, a0_ref, a0t_ref, dyt_ref, act):
    wide = x_ref[0].astype(F32)
    a0 = (wide * scale_of(wide)).astype(BF16)
    a0_ref[...] = a0
    ff = wg_ref.shape[2]
    for f in range(0, ff, CUT):
        gate = dot(a0, wg_ref[0, :, f : f + CUT])
        up = dot(a0, wu_ref[0, :, f : f + CUT])
        act[:, f : f + CUT] = (gate * jax.nn.sigmoid(gate) * up).astype(BF16)
    a0t_ref[...] = a0.T
    dyt_ref[...] = dy_ref[0].T
    h = x_ref[0] + dot(act[...], wd_ref[0]).astype(BF16)
    h_ref[...] = h
    wide = h.astype(F32)
    a1 = (wide * scale_of(wide)).astype(BF16)
    a1_ref[...] = a1
    a1t_ref[...] = a1.T


def forward(x, dy, wg, wu, wd, layer):
    _, tokens, d = x.shape
    ff = wg.shape[2]
    weight = lambda w: pl.BlockSpec((1,) + w.shape[1:], lambda i: (layer, 0, 0))
    seq = pl.BlockSpec((1, ROWS, d), lambda i: (0, i, 0))
    flat = pl.BlockSpec((ROWS, d), lambda i: (i, 0))
    turned = pl.BlockSpec((d, ROWS), lambda i: (0, i))
    plain, turn = jax.ShapeDtypeStruct((tokens, d), BF16), jax.ShapeDtypeStruct((d, tokens), BF16)
    return pl.pallas_call(
        forward_kernel,
        grid=(tokens // ROWS,),
        in_specs=[seq, seq, weight(wg), weight(wu), weight(wd)],
        out_specs=[flat, flat, turned, flat, turned, turned],
        out_shape=[plain, plain, turn, plain, turn, turn],
        scratch_shapes=[pltpu.VMEM((ROWS, ff), BF16)],
        compiler_params=pltpu.CompilerParams(vmem_limit_bytes=LIMIT),
        cost_estimate=pl.CostEstimate(flops=6 * tokens * d * ff, bytes_accessed=16 * tokens * d + 6 * d * ff, transcendentals=tokens * ff),
        name="forward",
    )(x, dy, wg, wu, wd)


def rdma(n, me, d, s, slot, own, landed, send_sem, recv_sem):
    turn = 1 - 2 * d
    shard = lax.rem(me - turn * s + 2 * n, n)
    high = own.shape[1] // (2 * n)
    mine = own.at[slot, pl.ds(pl.multiple_of((2 * shard + d) * high, 16), high), :]
    return mine, pltpu.make_async_remote_copy(
        src_ref=mine,
        dst_ref=landed.at[d, slot, s] if s < n - 1 else mine,
        send_sem=send_sem.at[d, slot],
        recv_sem=recv_sem.at[d, slot, s],
        device_id={"dp": lax.rem(me + turn + n, n)},
        device_id_type=pl.DeviceIdType.MESH,
    )


def backward_kernel(n, ringed, *refs):
    a1_in, a1t_in, dy_in, dyt_in, h_in, a0_in, a0t_in, wg_in, wu_in, wd_in = refs[:10]
    ring_out, direct_out = refs[10:12]
    a, at, dy, dyt, by_gate, by_up, own, landed, act, dgate, dup, wg, wu, wd = refs[12:26]
    load_sem, weight_sem, out_sem, send_sem, recv_sem = refs[26:]
    tokens, d_model = a.shape
    per = wg_in.shape[2] // TILE
    pieces = 2 * per
    me = lax.axis_index("dp")
    barrier = pltpu.get_barrier_semaphore()
    for other in (1, n - 1):
        pl.semaphore_signal(barrier, inc=1, device_id={"dp": lax.rem(me + other, n)}, device_id_type=pl.DeviceIdType.MESH)

    def load(pairs):
        copies = [pltpu.make_async_copy(src, dst, load_sem.at[i]) for i, (src, dst) in enumerate(pairs)]
        for copy in copies:
            copy.start()
        for copy in copies:
            copy.wait()

    def tiles(piece):
        which, slot = 1 - piece // per, lax.rem(piece, 2)
        here = pl.ds(pl.multiple_of(lax.rem(piece, per) * TILE, TILE), TILE)
        return [
            pltpu.make_async_copy(wg_in.at[which, :, here], wg.at[slot], weight_sem.at[slot, 0]),
            pltpu.make_async_copy(wu_in.at[which, :, here], wu.at[slot], weight_sem.at[slot, 1]),
            pltpu.make_async_copy(wd_in.at[which, here, :], wd.at[slot], weight_sem.at[slot, 2]),
        ]

    for copy in tiles(0):
        copy.start()
    load([(a1_in, a), (dy_in.at[0], dy), (a1t_in, at), (dyt_in, dyt)])
    by_gate[...] = jnp.zeros_like(by_gate)
    by_up[...] = jnp.zeros_like(by_up)
    pl.semaphore_wait(barrier, 2)

    def serve(turn, odd):
        for age in reversed(range(odd, n)):
            s = 2 * age - odd
            piece = turn - age

            @pl.when(jnp.logical_and(piece >= 0, piece < ringed))
            def _():
                slot = lax.rem(piece, n)
                for d in range(2):
                    if s:
                        before = rdma(n, me, d, s - 1, slot, own, landed, send_sem, recv_sem)[1]
                        before.wait_recv()
                        before.wait_send()
                    if s < 2 * n - 2:
                        mine, copy = rdma(n, me, d, s, slot, own, landed, send_sem, recv_sem)
                        if 0 < s < n:
                            mine[...] = (mine[...].astype(F32) + landed[d, slot, s - 1].astype(F32)).astype(BF16)
                        copy.start()
                if s == 2 * n - 2:
                    pltpu.make_async_copy(own.at[slot], ring_out.at[piece], out_sem.at[slot]).start()

    @pl.loop(0, max(pieces, ringed + n - 1))
    def _(turn):
        busy = turn < pieces
        slot = lax.rem(turn, n)
        now = lax.rem(turn, 2)

        @pl.when(turn == per)
        def _():
            load([(h_in, a)])

            @pl.loop(0, tokens // TILE)
            def _(c):
                here = pl.ds(pl.multiple_of(c * TILE, TILE), TILE)
                by_a = (by_gate[here, :].astype(BF16) + by_up[here, :].astype(BF16)).astype(F32)
                wide = a[here, :].astype(F32)
                scale = scale_of(wide)
                along = jnp.mean(by_a * wide, -1, keepdims=True)
                by_h = (by_a * scale - wide * (scale * scale * scale * along)).astype(BF16) + dy[here, :]
                dy[here, :] = by_h
                dyt[:, here] = by_h.T

            load([(a0_in, a), (a0t_in, at)])

        @pl.when(busy)
        def _():
            for copy in tiles(turn):
                copy.wait()

            @pl.when(turn + 1 < pieces)
            def _():
                for copy in tiles(turn + 1):
                    copy.start()

            @pl.loop(0, tokens // ROWS)
            def _(c):
                here = pl.ds(pl.multiple_of(c * ROWS, ROWS), ROWS)
                gate = dot(a[here, :], wg[now])
                up = dot(a[here, :], wu[now])
                by_act = dot_nt(dy[here, :], wd[now]).astype(BF16).astype(F32)
                sig = jax.nn.sigmoid(gate)
                silu = gate * sig
                act[here, :] = (silu * up).astype(BF16)
                dup[here, :] = (by_act * silu).astype(BF16)
                dgate[here, :] = (by_act * up * (sig + silu * (1 - sig))).astype(BF16)

        serve(turn, 1)

        @pl.when(busy)
        def _():
            @pl.when(turn >= n)
            def _():
                pltpu.make_async_copy(own.at[slot], ring_out.at[0], out_sem.at[slot]).wait()

            own[slot, :d_model, :] = dot(at[...], dgate[...]).astype(BF16)
            own[slot, d_model : 2 * d_model, :] = dot(at[...], dup[...]).astype(BF16)
            down = dot(dyt[...], act[...]).astype(BF16).T
            for i in range(d_model // TILE):
                own[slot, 2 * d_model + i * TILE : 2 * d_model + (i + 1) * TILE, :] = down[:, i * TILE : (i + 1) * TILE]

            @pl.when(turn >= ringed)
            def _():
                pltpu.make_async_copy(own.at[slot], direct_out.at[turn - ringed], out_sem.at[slot]).start()

        serve(turn, 0)

        @pl.when(turn < per)
        def _():
            @pl.loop(0, tokens // ROWS)
            def _(c):
                here = pl.ds(pl.multiple_of(c * ROWS, ROWS), ROWS)
                by_gate[here, :] += dot_nt(dgate[here, :], wg[now])
                by_up[here, :] += dot_nt(dup[here, :], wu[now])

    for slot in range(n):
        pltpu.make_async_copy(own.at[slot], ring_out.at[0], out_sem.at[slot]).wait()


def backward(n, x, dy, h1, a1, a1t, a0, a0t, dyt, wg, wu, wd):
    tokens, d = a1.shape
    ff = wg.shape[2]
    pieces = 2 * ff // TILE
    ringed = pieces - DIRECT
    high = 3 * d // (2 * n)
    anywhere = pl.BlockSpec(memory_space=pl.ANY)
    return pl.pallas_call(
        functools.partial(backward_kernel, n, ringed),
        in_specs=[anywhere] * 10,
        out_specs=[anywhere] * 2,
        out_shape=[jax.ShapeDtypeStruct((ringed, 3 * d, TILE), BF16), jax.ShapeDtypeStruct((DIRECT, 3 * d, TILE), BF16)],
        scratch_shapes=[
            pltpu.VMEM((tokens, d), BF16),
            pltpu.VMEM((d, tokens), BF16),
            pltpu.VMEM((tokens, d), BF16),
            pltpu.VMEM((d, tokens), BF16),
            pltpu.VMEM((tokens, d), F32),
            pltpu.VMEM((tokens, d), F32),
            pltpu.VMEM((n, 3 * d, TILE), BF16),
            pltpu.VMEM((2, n, n - 1, high, TILE), BF16),
            pltpu.VMEM((tokens, TILE), BF16),
            pltpu.VMEM((tokens, TILE), BF16),
            pltpu.VMEM((tokens, TILE), BF16),
            pltpu.VMEM((2, d, TILE), BF16),
            pltpu.VMEM((2, d, TILE), BF16),
            pltpu.VMEM((2, TILE, d), BF16),
            pltpu.SemaphoreType.DMA((4,)),
            pltpu.SemaphoreType.DMA((2, 3)),
            pltpu.SemaphoreType.DMA((n,)),
            pltpu.SemaphoreType.DMA((2, n)),
            pltpu.SemaphoreType.DMA((2, n, 2 * n - 2)),
        ],
        compiler_params=pltpu.CompilerParams(vmem_limit_bytes=63 * 1024 * 1024, collective_id=0, has_side_effects=True),
        cost_estimate=pl.CostEstimate(flops=28 * tokens * d * ff, bytes_accessed=40 * d * ff, transcendentals=2 * tokens * ff),
        name="backward",
    )(a1, a1t, dy, dyt, h1, a0, a0t, wg, wu, wd)


def adamw_kernel(*refs):
    ins, g_ref, outs = refs[:9], refs[9], refs[-9:]
    d = ins[0].shape[1]
    for i in range(3):
        w, m, v = (ins[3 * k + i] for k in range(3))
        if i < 2:
            g = g_ref[0, i * d : (i + 1) * d, :].astype(F32)
        else:
            g = jnp.concatenate([g_ref[0, at : at + TILE, :].astype(F32) for at in range(2 * d, 3 * d, TILE)], axis=1)
        new_m = 0.9 * m[0] + 0.1 * g
        new_v = 0.95 * v[0] + 0.05 * g * g
        step = new_m * lax.rsqrt(new_v + 1e-8) + 0.1 * w[0].astype(F32)
        outs[i][0] = (w[0].astype(F32) - 0.02 * step).astype(BF16)
        outs[3 + i][0] = new_m
        outs[6 + i][0] = new_v


def adamw(weights, ms, vs, g, so_far, first):
    d, ff = weights[0].shape[1:]
    per = ff // TILE
    which = lambda i: 1 - (first + i) // per
    col = pl.BlockSpec((1, d, TILE), lambda i: (which(i), 0, (first + i) % per))
    row = pl.BlockSpec((1, TILE, d), lambda i: (which(i), (first + i) % per, 0))
    three = [col, col, row]
    old = list(so_far or ())
    count = g.size
    return pl.pallas_call(
        adamw_kernel,
        grid=(g.shape[0],),
        in_specs=three * 3 + [pl.BlockSpec((1, 3 * d, TILE), lambda i: (i, 0, 0))] + [pl.BlockSpec(memory_space=pl.ANY)] * len(old),
        out_specs=three * 3,
        out_shape=[jax.ShapeDtypeStruct(v.shape, v.dtype) for v in (*weights, *ms, *vs)],
        input_output_aliases={10 + i: i for i in range(len(old))},
        compiler_params=pltpu.CompilerParams(vmem_limit_bytes=LIMIT),
        cost_estimate=pl.CostEstimate(flops=15 * count, bytes_accessed=22 * count, transcendentals=count),
        name=f"adamw_{first}",
    )(*weights, *ms, *vs, g, *old)


def solution(mesh):
    n = mesh.shape["dp"]

    def step(x, dy, *arrays):
        weights, ms, vs = (arrays[i : i + 3] for i in (0, 3, 6))
        wg, wu, wd = weights
        h1, a1, a1t, a0, a0t, dyt = forward(x, dy, wg, wu, wd, 0)
        ring, direct = backward(n, x, dy, h1, a1, a1t, a0, a0t, dyt, wg, wu, wd)
        direct = lax.psum(direct, "dp")
        so_far = adamw(weights, ms, vs, ring, None, 0)
        return tuple(adamw(weights, ms, vs, direct, so_far, ring.shape[0]))

    return jax.shard_map(
        step,
        mesh=mesh,
        in_specs=(P(("rep", "dp"), None, None),) * 2 + (P(None, None, None),) * 9,
        out_specs=(P("rep", None, None),) * 9,
        check_vma=False,
    )
```

time: 696 us -> 484 us (0.70)
  Pallas kernels: 0 us -> 440 us
  waiting for transfers between devices: 383 us -> 27.6 us
  matrix products: 209 us -> 0 us
  other arithmetic: 72.6 us -> 0 us
  local copies, waits for them, and re-layouts: 9.93 us -> 0 us
    pallas_call x0 -> x4, Pallas kernels: none -> 440 us  [the longest x1 341 us: backward(): pl.pallas_call(functools.partial(backward_kernel, n, ringed), in_specs=[a...]
    psum x1, waiting for transfers between devices: 383 us -> 27.6 us  [step(): direct = lax.psum(direct, 'dp')]
    dot_general x15 -> x0, matrix products: 209 us -> none  [the longest x5 78.2 us: layer(): gate = jnp.dot(a, w['w_gate'], preferred_element_type=jnp.float32)]
    convert_element_type x2 -> x0, other arithmetic: 66.7 us -> none  [adamw(): return ((w - 0.02 * step).astype(jnp.bfloat16), m, v)]
    unnamed x36 -> x0, local copies, waits for them, and re-layouts: 9.93 us -> none
  transfers between devices with their start and end apart: 1 -> 1, of which waited for: 1 -> 1; matrix products, arithmetic and copies ran while one was open for 0% -> 0% of each run, Pallas kernels for 0% -> 13%
where the time goes in v1:
time: 484 us; the launch traced here: 481 us
  Pallas kernels  440 us (91%)
  waiting for transfers between devices  27.6 us (6%)
  between operations  14.1 us (3%)
    pallas_call x1, Pallas kernels, backward(): pl.pallas_call(functools.partial(backward_kernel, n, ringed), in_specs=[a...  341 us
    pallas_call x2, Pallas kernels, adamw(): pl.pallas_call(adamw_kernel, grid=(g.shape[0],), in_specs=three * 3 + [pl...  69.2 us
    pallas_call x1, Pallas kernels, forward(): pl.pallas_call(forward_kernel, grid=(tokens // ROWS,), in_specs=[seq, seq...  29.3 us
    psum x1, waiting for transfers between devices, step(): direct = lax.psum(direct, 'dp')  27.6 us
  transfers between devices with their start and end apart: 1, of which 1 were waited for; matrix products, arithmetic and copies ran while one was open for 0% of the time, Pallas kernels for 13%

profile of v1, /device:TPU:21, one launch (start us, length us, event | category | flops | bytes accessed | tf_op | source)
XLA Modules:
  0.0 481.4 jit_solution(1858324901926863314)
XLA Ops:
  7.2 0.1 all-reduce.2.cloned.1.call-start
  7.3 29.3 %forward.1 = (bf16[2048,768]{1,0:T(8,128)(2,1)}, bf16[2048,768]{1,0:T(8,128)(2,1)}, bf16[768,2048]{1,0:T(8,128)(2,1)}, bf16[2048,768]{1,0:T(8,128)(2,1)}, bf16[7...) custom-call(bf16[1,2048,768]{2,1,0:T(8,128)(2,1)} %x_ref.1, bf16[1,2048,768]{2,1,0:T(8,128)(2,1)} %refs_2_.3, ...), custom_call_target="tpu_custom_call" | custom-call | flops 19327352832 | bytes 34603008 | tf_op jit(solution)/shard_map/forward/pallas_call | solution.py:58
  36.5 341.1 %backward.1 = (bf16[14,2304,256]{2,1,0:T(8,128)(2,1)}, bf16[2,2304,256]{2,1,0:T(8,128)(2,1)}) custom-call(bf16[2048,768]{1,0:T(8,128)(2,1)} %get-tuple-element.26.refs_0_, bf16[768,2048]{1,0:T(8,128)(2,1)} %get-tuple-element.27.refs_1_, bf16[1,2048,768]{2,1,0:T(8,128)(2,1)} %refs_2_.3, bf16[768,2048]{1,0:T(8,128)(2,1)} %get-tuple-element.28.refs_3_, ...), custom_call_target="tpu_custom_call" | custom-call | flops 90194313216 | bytes 62914560 | tf_op jit(solution)/shard_map/backward/pallas_call | solution.py:227
  377.7 0.1 all-reduce.2.cloned.1.call-update
  377.8 60.2 %adamw_0.1 = (bf16[2,768,2048]{2,1,0:T(8,128)(2,1)}, bf16[2,768,2048]{2,1,0:T(8,128)(2,1)}, bf16[2,2048,768]{2,1,0:T(8,128)(2,1)}, f32[2,768,2048]{2,1,0:T(8,128...) custom-call(bf16[2,768,2048]{2,1,0:T(8,128)(2,1)} %refs_0_.3, ...), custom_call_target="tpu_custom_call" | custom-call | flops 123863040 | bytes 181665792 | tf_op jit(solution)/shard_map/adamw_0/pallas_call | solution.py:285
  438.0 27.6 %all-reduce.2.cloned.1.call-done.refs_9_ = bf16[2,2304,256]{2,1,0:T(8,128)(2,1)} async-done(((bf16[2,2304,256]{2,1,0:T(8,128)(2,1)}), bf16[2,2304,256]{2,1,0:T(8,128)(2,1)}) %all-reduce.2.cloned.1.call-update) | async-done | bytes 2359312 | tf_op jit(solution)/shard_map/psum | solution.py:306
  465.6 8.9 %adamw_14.1 = (bf16[2,768,2048]{2,1,0:T(8,128)(2,1)}, bf16[2,768,2048]{2,1,0:T(8,128)(2,1)}, bf16[2,2048,768]{2,1,0:T(8,128)(2,1)}, f32[2,768,2048]{2,1,0:T(8,12...) custom-call(bf16[2,768,2048]{2,1,0:T(8,128)(2,1)} %refs_0_.3, ...), custom_call_target="tpu_custom_call", output_to_operand_aliasing={{0}: (10, {}), {1}: (11, {}), {2}: (12, {}), {3}: (13, {}),... | custom-call | flops 17694720 | bytes 25952256 | tf_op jit(solution)/shard_map/adamw_14/pallas_call | solution.py:285
Async XLA Ops:
  7.2 458.4 %all-reduce.2.cloned.1.call-start = ((), (), s32[]{:S(2)}) async-start(), calls=%async_computation | async-start | bytes 4718592 | tf_op jit(solution)/shard_map/psum | solution.py:306
Sparse Core Ops, SparseCore 0:
  377.9 87.6 all-reduce.1

commit v2 on v1

--- a/solution.py
+++ b/solution.py
@@ -12,7 +12,7 @@
 ROWS = 512
 CUT = 512
 TILE = 256
-DIRECT = 2
+DIRECT = 4
 NT = (((1,), (1,)), ((), ()))
 
 
@@ -68,17 +68,20 @@
     )(x, dy, wg, wu, wd)
 
 
-def rdma(n, me, d, s, slot, own, landed, send_sem, recv_sem):
-    turn = 1 - 2 * d
-    shard = lax.rem(me - turn * s + 2 * n, n)
+def ring_rows(n, me, d, s, slot, own):
+    shard = lax.rem(me - (1 - 2 * d) * s + 2 * n, n)
     high = own.shape[1] // (2 * n)
-    mine = own.at[slot, pl.ds(pl.multiple_of((2 * shard + d) * high, 16), high), :]
-    return mine, pltpu.make_async_remote_copy(
+    return own.at[slot, pl.ds(pl.multiple_of((2 * shard + d) * high, 16), high), :]
+
+
+def ring_copy(n, me, d, s, *, slot, own, landed, send_sem, recv_sem, whole):
+    mine = ring_rows(n, me, d, s, slot, own)
+    return pltpu.make_async_remote_copy(
         src_ref=mine,
-        dst_ref=landed.at[d, slot, s] if s < n - 1 else mine,
+        dst_ref=mine if whole else landed.at[d, slot, s],
         send_sem=send_sem.at[d, slot],
         recv_sem=recv_sem.at[d, slot, s],
-        device_id={"dp": lax.rem(me + turn + n, n)},
+        device_id={"dp": lax.rem(me + 1 - 2 * d + n, n)},
         device_id_type=pl.DeviceIdType.MESH,
     )
 
@@ -87,7 +90,7 @@
     a1_in, a1t_in, dy_in, dyt_in, h_in, a0_in, a0t_in, wg_in, wu_in, wd_in = refs[:10]
     ring_out, direct_out = refs[10:12]
     a, at, dy, dyt, by_gate, by_up, own, landed, act, dgate, dup, wg, wu, wd = refs[12:26]
-    load_sem, weight_sem, out_sem, send_sem, recv_sem = refs[26:]
+    load_sem, weight_sem, out_sem, direct_sem, send_sem, recv_sem = refs[26:]
     tokens, d_model = a.shape
     per = wg_in.shape[2] // TILE
     pieces = 2 * per
@@ -95,13 +98,6 @@
     barrier = pltpu.get_barrier_semaphore()
     for other in (1, n - 1):
         pl.semaphore_signal(barrier, inc=1, device_id={"dp": lax.rem(me + other, n)}, device_id_type=pl.DeviceIdType.MESH)
-
-    def load(pairs):
-        copies = [pltpu.make_async_copy(src, dst, load_sem.at[i]) for i, (src, dst) in enumerate(pairs)]
-        for copy in copies:
-            copy.start()
-        for copy in copies:
-            copy.wait()
 
     def tiles(piece):
         which, slot = 1 - piece // per, lax.rem(piece, 2)
@@ -114,33 +110,53 @@
 
     for copy in tiles(0):
         copy.start()
-    load([(a1_in, a), (dy_in.at[0], dy), (a1t_in, at), (dyt_in, dyt)])
+    plain = [pltpu.make_async_copy(a1_in, a, load_sem.at[0]), pltpu.make_async_copy(dy_in.at[0], dy, load_sem.at[1])]
+    turned = [pltpu.make_async_copy(a1t_in, at, load_sem.at[2]), pltpu.make_async_copy(dyt_in, dyt, load_sem.at[3])]
+    between = [pltpu.make_async_copy(src, dst, load_sem.at[i]) for i, (src, dst) in enumerate([(h_in, a), (a0t_in, at), (a0_in, a)])]
+    for copy in plain + turned:
+        copy.start()
     by_gate[...] = jnp.zeros_like(by_gate)
     by_up[...] = jnp.zeros_like(by_up)
+    for copy in plain:
+        copy.wait()
     pl.semaphore_wait(barrier, 2)
 
     def serve(turn, odd):
         for age in reversed(range(odd, n)):
-            s = 2 * age - odd
+            step = 2 * age - odd
             piece = turn - age
 
-            @pl.when(jnp.logical_and(piece >= 0, piece < ringed))
+            @pl.when(jnp.logical_and(piece >= 0, piece < (pieces if step < n else ringed)))
             def _():
                 slot = lax.rem(piece, n)
+                copy_of = functools.partial(ring_copy, n, me, slot=slot, own=own, landed=landed, send_sem=send_sem, recv_sem=recv_sem)
                 for d in range(2):
-                    if s:
-                        before = rdma(n, me, d, s - 1, slot, own, landed, send_sem, recv_sem)[1]
+                    if step:
+                        before = copy_of(d, step - 1, whole=step >= n)
                         before.wait_recv()
                         before.wait_send()
-                    if s < 2 * n - 2:
-                        mine, copy = rdma(n, me, d, s, slot, own, landed, send_sem, recv_sem)
-                        if 0 < s < n:
-                            mine[...] = (mine[...].astype(F32) + landed[d, slot, s - 1].astype(F32)).astype(BF16)
-                        copy.start()
-                if s == 2 * n - 2:
+                    mine = ring_rows(n, me, d, step, slot, own)
+                    if 0 < step < n:
+                        mine[...] = (mine[...].astype(F32) + landed[d, slot, step - 1].astype(F32)).astype(BF16)
+                    if step < n - 1:
+                        copy_of(d, step, whole=False).start()
+                    elif step > n - 1 and step < 2 * n - 2:
+                        copy_of(d, step, whole=True).start()
+                    elif step == n - 1:
+
+                        @pl.when(piece < ringed)
+                        def _():
+                            copy_of(d, step, whole=True).start()
+
+                        @pl.when(piece >= ringed)
+                        def _():
+                            at_out = piece - ringed
+                            pltpu.make_async_copy(mine, direct_out.at[at_out, d], direct_sem.at[at_out, d]).start()
+
+                if step == 2 * n - 2:
                     pltpu.make_async_copy(own.at[slot], ring_out.at[piece], out_sem.at[slot]).start()
 
-    @pl.loop(0, max(pieces, ringed + n - 1))
+    @pl.loop(0, max(pieces + n // 2, ringed + n - 1))
     def _(turn):
         busy = turn < pieces
         slot = lax.rem(turn, n)
@@ -148,7 +164,8 @@
 
         @pl.when(turn == per)
         def _():
-            load([(h_in, a)])
+            between[0].wait()
+            between[1].start()
 
             @pl.loop(0, tokens // TILE)
             def _(c):
@@ -161,7 +178,10 @@
                 dy[here, :] = by_h
                 dyt[:, here] = by_h.T
 
-            load([(a0_in, a), (a0t_in, at)])
+            between[2].start()
+            serve(turn, 1)
+            between[1].wait()
+            between[2].wait()
 
         @pl.when(busy)
         def _():
@@ -173,9 +193,8 @@
                 for copy in tiles(turn + 1):
                     copy.start()
 
-            @pl.loop(0, tokens // ROWS)
-            def _(c):
-                here = pl.ds(pl.multiple_of(c * ROWS, ROWS), ROWS)
+            for at_row in range(0, tokens, ROWS):
+                here = pl.ds(at_row, ROWS)
                 gate = dot(a[here, :], wg[now])
                 up = dot(a[here, :], wu[now])
                 by_act = dot_nt(dy[here, :], wd[now]).astype(BF16).astype(F32)
@@ -185,7 +204,16 @@
                 dup[here, :] = (by_act * silu).astype(BF16)
                 dgate[here, :] = (by_act * up * (sig + silu * (1 - sig))).astype(BF16)
 
-        serve(turn, 1)
+        @pl.when(turn == per - 1)
+        def _():
+            between[0].start()
+
+        pl.when(turn != per)(functools.partial(serve, turn, 1))
+
+        @pl.when(turn == 0)
+        def _():
+            for copy in turned:
+                copy.wait()
 
         @pl.when(busy)
         def _():
@@ -199,22 +227,23 @@
             for i in range(d_model // TILE):
                 own[slot, 2 * d_model + i * TILE : 2 * d_model + (i + 1) * TILE, :] = down[:, i * TILE : (i + 1) * TILE]
 
-            @pl.when(turn >= ringed)
-            def _():
-                pltpu.make_async_copy(own.at[slot], direct_out.at[turn - ringed], out_sem.at[slot]).start()
-
-        serve(turn, 0)
-
-        @pl.when(turn < per)
-        def _():
+        def by_input():
             @pl.loop(0, tokens // ROWS)
             def _(c):
                 here = pl.ds(pl.multiple_of(c * ROWS, ROWS), ROWS)
                 by_gate[here, :] += dot_nt(dgate[here, :], wg[now])
                 by_up[here, :] += dot_nt(dup[here, :], wu[now])
 
-    for slot in range(n):
-        pltpu.make_async_copy(own.at[slot], ring_out.at[0], out_sem.at[slot]).wait()
+        pl.when(jnp.logical_and(turn > 0, turn < per))(by_input)
+        serve(turn, 0)
+        pl.when(turn == 0)(by_input)
+
+    for piece in range(pieces - n, ringed):
+        pltpu.make_async_copy(own.at[piece % n], ring_out.at[piece], out_sem.at[piece % n]).wait()
+    for piece in range(ringed, pieces):
+        for d in range(2):
+            rows = own.at[piece % n, : own.shape[1] // (2 * n), :]
+            pltpu.make_async_copy(rows, direct_out.at[piece - ringed, d], direct_sem.at[piece - ringed, d]).wait()
 
 
 def backward(n, x, dy, h1, a1, a1t, a0, a0t, dyt, wg, wu, wd):
@@ -228,7 +257,7 @@
         functools.partial(backward_kernel, n, ringed),
         in_specs=[anywhere] * 10,
         out_specs=[anywhere] * 2,
-        out_shape=[jax.ShapeDtypeStruct((ringed, 3 * d, TILE), BF16), jax.ShapeDtypeStruct((DIRECT, 3 * d, TILE), BF16)],
+        out_shape=[jax.ShapeDtypeStruct((ringed, 3 * d, TILE), BF16), jax.ShapeDtypeStruct((DIRECT, 2, high, TILE), BF16)],
         scratch_shapes=[
             pltpu.VMEM((tokens, d), BF16),
             pltpu.VMEM((d, tokens), BF16),
@@ -247,6 +276,7 @@
             pltpu.SemaphoreType.DMA((4,)),
             pltpu.SemaphoreType.DMA((2, 3)),
             pltpu.SemaphoreType.DMA((n,)),
+            pltpu.SemaphoreType.DMA((DIRECT, 2)),
             pltpu.SemaphoreType.DMA((2, n)),
             pltpu.SemaphoreType.DMA((2, n, 2 * n - 2)),
         ],
@@ -257,14 +287,21 @@
 
 
 def adamw_kernel(*refs):
-    ins, g_ref, outs = refs[:9], refs[9], refs[-9:]
+    ins, shards, outs, whole = refs[:9], refs[9], refs[-10:-1], refs[-1]
     d = ins[0].shape[1]
+    if len(shards.shape) == 3:
+        g_ref = shards.at[0]
+    else:
+        g_ref, (n, _, _, high, _) = whole, shards.shape
+        for q in range(n):
+            g_ref[2 * q * high : (2 * q + 1) * high, :] = shards[(q - 1) % n, 0, 0]
+            g_ref[(2 * q + 1) * high : (2 * q + 2) * high, :] = shards[(q + 1) % n, 0, 1]
     for i in range(3):
         w, m, v = (ins[3 * k + i] for k in range(3))
         if i < 2:
-            g = g_ref[0, i * d : (i + 1) * d, :].astype(F32)
+            g = g_ref[i * d : (i + 1) * d, :].astype(F32)
         else:
-            g = jnp.concatenate([g_ref[0, at : at + TILE, :].astype(F32) for at in range(2 * d, 3 * d, TILE)], axis=1)
+            g = jnp.concatenate([g_ref[at : at + TILE, :].astype(F32) for at in range(2 * d, 3 * d, TILE)], axis=1)
         new_m = 0.9 * m[0] + 0.1 * g
         new_v = 0.95 * v[0] + 0.05 * g * g
         step = new_m * lax.rsqrt(new_v + 1e-8) + 0.1 * w[0].astype(F32)
@@ -282,13 +319,18 @@
     three = [col, col, row]
     old = list(so_far or ())
     count = g.size
+    if g.ndim == 3:
+        number, spec = g.shape[0], pl.BlockSpec((1, 3 * d, TILE), lambda i: (i, 0, 0))
+    else:
+        number, spec = g.shape[1], pl.BlockSpec((g.shape[0], 1, *g.shape[2:]), lambda i: (0, i, 0, 0, 0))
     return pl.pallas_call(
         adamw_kernel,
-        grid=(g.shape[0],),
-        in_specs=three * 3 + [pl.BlockSpec((1, 3 * d, TILE), lambda i: (i, 0, 0))] + [pl.BlockSpec(memory_space=pl.ANY)] * len(old),
+        grid=(number,),
+        in_specs=three * 3 + [spec] + [pl.BlockSpec(memory_space=pl.ANY)] * len(old),
         out_specs=three * 3,
         out_shape=[jax.ShapeDtypeStruct(v.shape, v.dtype) for v in (*weights, *ms, *vs)],
         input_output_aliases={10 + i: i for i in range(len(old))},
+        scratch_shapes=[pltpu.VMEM((3 * d, TILE), BF16)],
         compiler_params=pltpu.CompilerParams(vmem_limit_bytes=LIMIT),
         cost_estimate=pl.CostEstimate(flops=15 * count, bytes_accessed=22 * count, transcendentals=count),
         name=f"adamw_{first}",
@@ -303,7 +345,7 @@
         wg, wu, wd = weights
         h1, a1, a1t, a0, a0t, dyt = forward(x, dy, wg, wu, wd, 0)
         ring, direct = backward(n, x, dy, h1, a1, a1t, a0, a0t, dyt, wg, wu, wd)
-        direct = lax.psum(direct, "dp")
+        direct = lax.all_gather(direct, "dp")
         so_far = adamw(weights, ms, vs, ring, None, 0)
         return tuple(adamw(weights, ms, vs, direct, so_far, ring.shape[0]))
 

time: 484 us -> 465 us (0.961)
  waiting for transfers between devices: 27.6 us -> 11.1 us
    psum x1 -> x0, waiting for transfers between devices: 27.6 us -> none  [step(): direct = lax.psum(direct, 'dp')]
    all_gather x0 -> x1, waiting for transfers between devices: none -> 11.1 us  [step(): direct = lax.all_gather(direct, 'dp')]
  transfers between devices with their start and end apart: 1 -> 1, of which waited for: 1 -> 1; matrix products, arithmetic and copies ran while one was open for 0% -> 0% of each run, Pallas kernels for 13% -> 11%
where the time goes in v2:
time: 465 us
  Pallas kernels  440 us (95%)
  between operations  14.1 us (3%)
  waiting for transfers between devices  11.1 us (2%)
    pallas_call x1, Pallas kernels, backward(): pl.pallas_call(functools.partial(backward_kernel, n, ringed), in_specs=[a...  341 us
    pallas_call x2, Pallas kernels, adamw(): pl.pallas_call(adamw_kernel, grid=(number,), in_specs=three * 3 + [spec]...  69 us
    pallas_call x1, Pallas kernels, forward(): pl.pallas_call(forward_kernel, grid=(tokens // ROWS,), in_specs=[seq, seq...  29.3 us
    all_gather x1, waiting for transfers between devices, step(): direct = lax.all_gather(direct, 'dp')  11.1 us
  transfers between devices with their start and end apart: 1, of which 1 were waited for; matrix products, arithmetic and copies ran while one was open for 0% of the time, Pallas kernels for 11%

profile of v2, /device:TPU:21, one launch (start us, length us, event | category | flops | bytes accessed | tf_op | source)
XLA Modules:
  0.0 464.9 jit_solution(6531285129443027946)
XLA Ops:
  7.2 0.1 all-gather.3.cloned.1.call-start
  7.3 29.3 %forward.1 = (bf16[2048,768]{1,0:T(8,128)(2,1)}, bf16[2048,768]{1,0:T(8,128)(2,1)}, bf16[768,2048]{1,0:T(8,128)(2,1)}, bf16[2048,768]{1,0:T(8,128)(2,1)}, bf16[7...) custom-call(bf16[1,2048,768]{2,1,0:T(8,128)(2,1)} %x_ref.1, bf16[1,2048,768]{2,1,0:T(8,128)(2,1)} %refs_2_.3, ...), custom_call_target="tpu_custom_call" | custom-call | flops 19327352832 | bytes 34603008 | tf_op jit(solution)/shard_map/forward/pallas_call | solution.py:58
  36.5 341.3 %backward.1 = (bf16[12,2304,256]{2,1,0:T(8,128)(2,1)}, bf16[4,2,144,256]{3,2,1,0:T(8,128)(2,1)}) custom-call(bf16[2048,768]{1,0:T(8,128)(2,1)} %get-tuple-element.26.refs_0_, bf16[768,2048]{1,0:T(8,128)(2,1)} %get-tuple-element.27.refs_1_, bf16[1,2048,768]{2,1,0:T(8,128)(2,1)} %refs_2_.3, bf16[768,2048]{1,0:T(8,128)(2,1)} %get-tuple-element.28.refs_3_, ...), custom_call_target="tpu_custom_call" | custom-call | flops 90194313216 | bytes 62914560 | tf_op jit(solution)/shard_map/backward/pallas_call | solution.py:256
  377.9 0.1 all-gather.3.cloned.1.call-update
  377.9 51.5 %adamw_0.1 = (bf16[2,768,2048]{2,1,0:T(8,128)(2,1)}, bf16[2,768,2048]{2,1,0:T(8,128)(2,1)}, bf16[2,2048,768]{2,1,0:T(8,128)(2,1)}, f32[2,768,2048]{2,1,0:T(8,128...) custom-call(bf16[2,768,2048]{2,1,0:T(8,128)(2,1)} %refs_0_.3, ...), custom_call_target="tpu_custom_call" | custom-call | flops 106168320 | bytes 155713536 | tf_op jit(solution)/shard_map/adamw_0/pallas_call | solution.py:326
  429.5 11.1 %all-gather.3.cloned.1.call-done = bf16[32,2,144,256]{3,2,1,0:T(8,128)(2,1)} async-done(((bf16[4,2,144,256]{3,2,1,0:T(8,128)(2,1)}), bf16[32,2,144,256]{3,2,1,0:T(8,128)(2,1)}) %all-gather.3.cloned.1.call-update) | async-done | bytes 4718608 | tf_op jit(solution)/shard_map/all_gather | solution.py:348
  440.6 17.4 %adamw_12.1 = (bf16[2,768,2048]{2,1,0:T(8,128)(2,1)}, bf16[2,768,2048]{2,1,0:T(8,128)(2,1)}, bf16[2,2048,768]{2,1,0:T(8,128)(2,1)}, f32[2,768,2048]{2,1,0:T(8,12...) custom-call(bf16[2,768,2048]{2,1,0:T(8,128)(2,1)} %refs_0_.3, ...), custom_call_target="tpu_custom_call", output_to_operand_aliasing={{0}: (10, {}), {1}: (11, {}), {2}: (12, {}), {3}: (13, {}),... | custom-call | flops 35389440 | bytes 51904512 | tf_op jit(solution)/shard_map/adamw_12/pallas_call | solution.py:326
Async XLA Ops:
  7.2 433.4 %all-gather.3.cloned.1.call-start = ((), (), s32[]{:S(2)}) async-start(), calls=%async_computation | async-start | bytes 5308416 | tf_op jit(solution)/shard_map/all_gather | solution.py:348
Sparse Core Ops, SparseCore 0:
  378.1 62.4 all-gather.2
